TPU v7x, 8 devices: a whole 2x2x1 slice. The times are simulated.
8 devices in a mesh: stage: 2 (over z, y), expert: 4 (over x, core).
Axes of the slice: x: 2, y: 2, z: 1, core: 2. Of those that a mesh axis runs over, the one named last changes fastest.
Arguments:
- w_gate: bfloat16 [12, 16, 1024, 512], P('stage', 'expert')
- w_up: bfloat16 [12, 16, 1024, 512], P('stage', 'expert')
- w_down: bfloat16 [12, 16, 512, 1024], P('stage', 'expert')
- x: bfloat16 [2048, 1024], P(('stage', 'expert'))
- expert_ids: int32 [12, 2048, 8], P(None, ('stage', 'expert'))
- gates: float32 [12, 2048, 8], P(None, ('stage', 'expert'))
Outputs:
- output 1: bfloat16 [12, 16, 1024, 1024], P(None, ('stage', 'expert'))
- output 2: bfloat16 [12, 16, 512, 1024], P(None, ('stage', 'expert'))
- output 3: float32 [12, 2048, 1024], P(None, ('stage', 'expert'))
All inputs are finite; a program needn't handle non-finite values.
Results may differ from a plain program's by a relative error of at most 0.00555969.
Values are sent between devices in bfloat16 or wider.
A program may use at most 1 GiB of HBM per device.

v0:
```python
import jax
import jax.numpy as jnp
from jax import lax
from jax.sharding import PartitionSpec as P

NORM_EPS = 1e-6
FLAT = ("stage", "expert")


def norm_rows(hidden):
    return (hidden * lax.rsqrt(jnp.mean(hidden * hidden, axis=-1, keepdims=True) + NORM_EPS)).astype(jnp.bfloat16)


def slot_table(layer_ids, n_experts, capacity):
    flat_ids = layer_ids.reshape(-1)
    onehot = (flat_ids[:, None] == jnp.arange(n_experts)[None, :]).astype(jnp.int32)
    pair_rank = jnp.sum(onehot * jnp.cumsum(onehot, axis=0), axis=-1) - 1
    return flat_ids * capacity + pair_rank


def moe_layer(hidden, layer_w13, layer_down, layer_ids, layer_mix, capacity, dev_count):
    tok_dev, model_width = hidden.shape
    top_k = layer_ids.shape[-1]
    exp_dev = layer_w13.shape[0]
    expert_width = layer_down.shape[1]
    n_experts = exp_dev * dev_count
    normed = norm_rows(hidden)
    slot_pos = slot_table(layer_ids, n_experts, capacity)
    pair_tok = jnp.arange(tok_dev * top_k, dtype=jnp.int32) // top_k
    source_row = jnp.zeros((n_experts * capacity,), jnp.int32).at[slot_pos].set(pair_tok)
    outbound = jnp.take(normed, source_row, axis=0).reshape(dev_count, exp_dev, capacity, model_width)
    inbound = lax.all_to_all(outbound, FLAT, 0, 0, tiled=True)
    projected = jnp.einsum("nxcd,xdg->nxcg", inbound, layer_w13, preferred_element_type=jnp.float32)
    activated = (jax.nn.silu(projected[..., :expert_width]) * projected[..., expert_width:]).astype(jnp.bfloat16)
    expert_out = jnp.einsum("nxcf,xfd->nxcd", activated, layer_down, preferred_element_type=jnp.float32).astype(jnp.bfloat16)
    returned = lax.all_to_all(expert_out, FLAT, 0, 0, tiled=True)
    picked = jnp.take(returned.reshape(n_experts * capacity, model_width), slot_pos, axis=0)
    picked = picked.reshape(tok_dev, top_k, model_width).astype(jnp.float32)
    return hidden + jnp.sum(layer_mix[..., None] * picked, axis=1)


def hand_over(gate_loc, up_loc, down_loc, n_stage, n_group):
    stage_idx = lax.axis_index("stage")
    flat_idx = stage_idx * n_group + lax.axis_index("expert")
    lay_stage = gate_loc.shape[0]
    exp_dev = gate_loc.shape[1] // n_stage
    fused_loc = jnp.concatenate([gate_loc, up_loc], axis=-1)
    fused_new = jnp.zeros((lay_stage * n_stage, exp_dev) + fused_loc.shape[2:], fused_loc.dtype)
    down_new = jnp.zeros((lay_stage * n_stage, exp_dev) + down_loc.shape[2:], down_loc.dtype)
    for round_idx in range(n_stage):
        pair_list = [(src_stage * n_group + src_group, src_group * n_stage + (src_stage + round_idx) % n_stage) for src_stage in range(n_stage) for src_group in range(n_group)]
        piece_idx = (stage_idx + round_idx) % n_stage
        fused_in = lax.ppermute(lax.dynamic_slice_in_dim(fused_loc, piece_idx * exp_dev, exp_dev, axis=1), FLAT, pair_list)
        down_in = lax.ppermute(lax.dynamic_slice_in_dim(down_loc, piece_idx * exp_dev, exp_dev, axis=1), FLAT, pair_list)
        from_stage = (flat_idx % n_stage - round_idx) % n_stage
        fused_new = lax.dynamic_update_slice_in_dim(fused_new, fused_in, from_stage * lay_stage, axis=0)
        down_new = lax.dynamic_update_slice_in_dim(down_new, down_in, from_stage * lay_stage, axis=0)
    return fused_new, down_new


def solution(mesh):
    n_stage = mesh.shape["stage"]
    n_group = mesh.shape["expert"]
    dev_count = n_stage * n_group

    def per_device(gate_loc, up_loc, down_loc, x_loc, ids_loc, mix_loc):
        fused_new, down_new = hand_over(gate_loc, up_loc, down_loc, n_stage, n_group)
        n_experts = fused_new.shape[1] * dev_count
        capacity = 3 * x_loc.shape[0] * ids_loc.shape[-1] // (2 * n_experts)
        hidden = x_loc.astype(jnp.float32)
        layer_outs = []
        for layer_idx in range(fused_new.shape[0]):
            hidden = moe_layer(hidden, fused_new[layer_idx], down_new[layer_idx], ids_loc[layer_idx], mix_loc[layer_idx], capacity, dev_count)
            layer_outs.append(hidden)
        return fused_new, down_new, jnp.stack(layer_outs)

    weight_spec = P("stage", "expert")
    token_spec = P(None, FLAT)
    return jax.shard_map(per_device, mesh=mesh, in_specs=(weight_spec, weight_spec, weight_spec, P(FLAT), token_spec, token_spec), out_specs=(token_spec, token_spec, token_spec), check_vma=False)
```

profile of v0, /device:TPU:0, one launch (start us, length us, event | category | flops | bytes accessed | tf_op | source)
XLA Modules:
  0.0 3428.7 jit_solution(9295747547632314109)
XLA Ops:
  75.6 189.1 %collective-permute-start = (bf16[6,2,1024,1024]{3,2,1,0:T(8,128)(2,1)}, bf16[6,2,1024,1024]{3,2,1,0:T(8,128)(2,1)}, u32[]{:S(2)}, u32[]{:S(2)}) collective-permute-start(bf16[6,2,1024,1024]{3,2,1,0:T(8,128)(2,1)} %get-tuple-element.26), channel_id=1, source_target_pairs={{0,0},{1,2},{2,4},{3,6},{4,1},{5,3},{6,5},{7,7}} | collective-permute-start | bytes 75497480 | tf_op jit(solution)/shard_map/ppermute | solution.py:53
  282.2 95.3 %collective-permute-start.2 = (bf16[6,2,512,1024]{3,2,1,0:T(8,128)(2,1)}, bf16[6,2,512,1024]{3,2,1,0:T(8,128)(2,1)}, u32[]{:S(2)}, u32[]{:S(2)}) collective-permute-start(bf16[6,2,512,1024]{3,2,1,0:T(8,128)(2,1)} %get-tuple-element.28), channel_id=1, source_target_pairs={{0,0},{1,2},{2,4},{3,6},{4,1},{5,3},{6,5},{7,7}} | collective-permute-start | bytes 37748744 | tf_op jit(solution)/shard_map/ppermute | solution.py:54
  452.1 473.0 %collective-permute-done.3 = bf16[6,2,512,1024]{3,2,1,0:T(8,128)(2,1)} collective-permute-done((bf16[6,2,512,1024]{3,2,1,0:T(8,128)(2,1)}, bf16[6,2,512,1024]{3,2,1,0:T(8,128)(2,1)}, u32[]{:S(2)}, u32[]{:S(2)}) %collective-permute-start.3) | collective-permute-done | bytes 12582944 | tf_op jit(solution)/shard_map/ppermute | solution.py:54
  1029.4 71.2 %all-to-all-done.1 = bf16[8,2,192,1024]{3,2,1,0:T(8,128)(2,1)} async-done(((bf16[8,2,192,1024]{3,2,1,0:T(8,128)(2,1)}), bf16[8,2,192,1024]{3,2,1,0:T(8,128)(2,1)}, u32[]{:S(2)}, u32[]{:S(2)}) %all-to-all-start.1) | async-done | bytes 6291488 | tf_op jit(solution)/shard_map/all_to_all | solution.py:36
  1138.5 72.8 %all_to_all.120 = bf16[8,2,192,1024]{3,2,1,0:T(8,128)(2,1)S(1)} all-to-all(bf16[8,2,192,1024]{3,2,1,0:T(8,128)(2,1)S(1)} %bitcast.493), channel_id=1, replica_groups=mesh['stage'=2,'expert'=4] {'stage','expert'}, dimensions={0} | all-to-all | bytes 12582912 | tf_op jit(solution)/shard_map/all_to_all | solution.py:32
  1268.1 42.2 %all-to-all-done.3 = bf16[8,2,192,1024]{3,2,1,0:T(8,128)(2,1)} async-done(((bf16[8,2,192,1024]{3,2,1,0:T(8,128)(2,1)}), bf16[8,2,192,1024]{3,2,1,0:T(8,128)(2,1)}, u32[]{:S(2)}, u32[]{:S(2)}) %all-to-all-start.3) | async-done | bytes 6291488 | tf_op jit(solution)/shard_map/all_to_all | solution.py:36
  1348.4 73.0 %all_to_all.121 = bf16[8,2,192,1024]{3,2,1,0:T(8,128)(2,1)S(1)} all-to-all(bf16[8,2,192,1024]{3,2,1,0:T(8,128)(2,1)S(1)} %bitcast.494), channel_id=1, replica_groups=mesh['stage'=2,'expert'=4] {'stage','expert'}, dimensions={0} | all-to-all | bytes 12582912 | tf_op jit(solution)/shard_map/all_to_all | solution.py:32
  1448.5 71.3 %all-to-all-done.5 = bf16[8,2,192,1024]{3,2,1,0:T(8,128)(2,1)} async-done(((bf16[8,2,192,1024]{3,2,1,0:T(8,128)(2,1)}), bf16[8,2,192,1024]{3,2,1,0:T(8,128)(2,1)}, u32[]{:S(2)}, u32[]{:S(2)}) %all-to-all-start.5) | async-done | bytes 6291488 | tf_op jit(solution)/shard_map/all_to_all | solution.py:36
  1557.9 73.0 %all_to_all.122 = bf16[8,2,192,1024]{3,2,1,0:T(8,128)(2,1)S(1)} all-to-all(bf16[8,2,192,1024]{3,2,1,0:T(8,128)(2,1)S(1)} %bitcast.495), channel_id=1, replica_groups=mesh['stage'=2,'expert'=4] {'stage','expert'}, dimensions={0} | all-to-all | bytes 12582912 | tf_op jit(solution)/shard_map/all_to_all | solution.py:32
  1767.4 72.8 %all_to_all.123 = bf16[8,2,192,1024]{3,2,1,0:T(8,128)(2,1)S(1)} all-to-all(bf16[8,2,192,1024]{3,2,1,0:T(8,128)(2,1)S(1)} %bitcast.496), channel_id=1, replica_groups=mesh['stage'=2,'expert'=4] {'stage','expert'}, dimensions={0} | all-to-all | bytes 12582912 | tf_op jit(solution)/shard_map/all_to_all | solution.py:32
  1867.6 71.3 %all-to-all-done.9 = bf16[8,2,192,1024]{3,2,1,0:T(8,128)(2,1)} async-done(((bf16[8,2,192,1024]{3,2,1,0:T(8,128)(2,1)}), bf16[8,2,192,1024]{3,2,1,0:T(8,128)(2,1)}, u32[]{:S(2)}, u32[]{:S(2)}) %all-to-all-start.9) | async-done | bytes 6291488 | tf_op jit(solution)/shard_map/all_to_all | solution.py:36
  1976.9 72.8 %all_to_all.124 = bf16[8,2,192,1024]{3,2,1,0:T(8,128)(2,1)S(1)} all-to-all(bf16[8,2,192,1024]{3,2,1,0:T(8,128)(2,1)S(1)} %bitcast.497), channel_id=1, replica_groups=mesh['stage'=2,'expert'=4] {'stage','expert'}, dimensions={0} | all-to-all | bytes 12582912 | tf_op jit(solution)/shard_map/all_to_all | solution.py:32
  2106.3 42.2 %all-to-all-done.11 = bf16[8,2,192,1024]{3,2,1,0:T(8,128)(2,1)} async-done(((bf16[8,2,192,1024]{3,2,1,0:T(8,128)(2,1)}), bf16[8,2,192,1024]{3,2,1,0:T(8,128)(2,1)}, u32[]{:S(2)}, u32[]{:S(2)}) %all-to-all-start.11) | async-done | bytes 6291488 | tf_op jit(solution)/shard_map/all_to_all | solution.py:36
  2186.5 73.2 %all_to_all.125 = bf16[8,2,192,1024]{3,2,1,0:T(8,128)(2,1)S(1)} all-to-all(bf16[8,2,192,1024]{3,2,1,0:T(8,128)(2,1)S(1)} %bitcast.498), channel_id=1, replica_groups=mesh['stage'=2,'expert'=4] {'stage','expert'}, dimensions={0} | all-to-all | bytes 12582912 | tf_op jit(solution)/shard_map/all_to_all | solution.py:32
  2286.9 71.3 %all-to-all-done.13 = bf16[8,2,192,1024]{3,2,1,0:T(8,128)(2,1)} async-done(((bf16[8,2,192,1024]{3,2,1,0:T(8,128)(2,1)}), bf16[8,2,192,1024]{3,2,1,0:T(8,128)(2,1)}, u32[]{:S(2)}, u32[]{:S(2)}) %all-to-all-start.13) | async-done | bytes 6291488 | tf_op jit(solution)/shard_map/all_to_all | solution.py:36
  2396.2 73.0 %all_to_all.126 = bf16[8,2,192,1024]{3,2,1,0:T(8,128)(2,1)S(1)} all-to-all(bf16[8,2,192,1024]{3,2,1,0:T(8,128)(2,1)S(1)} %bitcast.499), channel_id=1, replica_groups=mesh['stage'=2,'expert'=4] {'stage','expert'}, dimensions={0} | all-to-all | bytes 12582912 | tf_op jit(solution)/shard_map/all_to_all | solution.py:32
  2605.7 72.8 %all_to_all.127 = bf16[8,2,192,1024]{3,2,1,0:T(8,128)(2,1)S(1)} all-to-all(bf16[8,2,192,1024]{3,2,1,0:T(8,128)(2,1)S(1)} %bitcast.500), channel_id=1, replica_groups=mesh['stage'=2,'expert'=4] {'stage','expert'}, dimensions={0} | all-to-all | bytes 12582912 | tf_op jit(solution)/shard_map/all_to_all | solution.py:32
  2706.1 71.3 %all-to-all-done.17 = bf16[8,2,192,1024]{3,2,1,0:T(8,128)(2,1)} async-done(((bf16[8,2,192,1024]{3,2,1,0:T(8,128)(2,1)}), bf16[8,2,192,1024]{3,2,1,0:T(8,128)(2,1)}, u32[]{:S(2)}, u32[]{:S(2)}) %all-to-all-start.17) | async-done | bytes 6291488 | tf_op jit(solution)/shard_map/all_to_all | solution.py:36
  2815.4 72.8 %all_to_all.128 = bf16[8,2,192,1024]{3,2,1,0:T(8,128)(2,1)S(1)} all-to-all(bf16[8,2,192,1024]{3,2,1,0:T(8,128)(2,1)S(1)} %bitcast.501), channel_id=1, replica_groups=mesh['stage'=2,'expert'=4] {'stage','expert'}, dimensions={0} | all-to-all | bytes 12582912 | tf_op jit(solution)/shard_map/all_to_all | solution.py:32
  2944.8 42.2 %all-to-all-done.19 = bf16[8,2,192,1024]{3,2,1,0:T(8,128)(2,1)} async-done(((bf16[8,2,192,1024]{3,2,1,0:T(8,128)(2,1)}), bf16[8,2,192,1024]{3,2,1,0:T(8,128)(2,1)}, u32[]{:S(2)}, u32[]{:S(2)}) %all-to-all-start.19) | async-done | bytes 6291488 | tf_op jit(solution)/shard_map/all_to_all | solution.py:36
  3026.0 73.0 %all_to_all.129 = bf16[8,2,192,1024]{3,2,1,0:T(8,128)(2,1)S(1)} all-to-all(bf16[8,2,192,1024]{3,2,1,0:T(8,128)(2,1)S(1)} %bitcast.502), channel_id=1, replica_groups=mesh['stage'=2,'expert'=4] {'stage','expert'}, dimensions={0} | all-to-all | bytes 12582912 | tf_op jit(solution)/shard_map/all_to_all | solution.py:32
  3126.2 71.3 %all-to-all-done.21 = bf16[8,2,192,1024]{3,2,1,0:T(8,128)(2,1)} async-done(((bf16[8,2,192,1024]{3,2,1,0:T(8,128)(2,1)}), bf16[8,2,192,1024]{3,2,1,0:T(8,128)(2,1)}, u32[]{:S(2)}, u32[]{:S(2)}) %all-to-all-start.21) | async-done | bytes 6291488 | tf_op jit(solution)/shard_map/all_to_all | solution.py:36
  3235.6 73.1 %all_to_all.130 = bf16[8,2,192,1024]{3,2,1,0:T(8,128)(2,1)S(1)} all-to-all(bf16[8,2,192,1024]{3,2,1,0:T(8,128)(2,1)S(1)} %bitcast.503), channel_id=1, replica_groups=mesh['stage'=2,'expert'=4] {'stage','expert'}, dimensions={0} | all-to-all | bytes 12582912 | tf_op jit(solution)/shard_map/all_to_all | solution.py:32
  3350.5 56.6 %all-to-all-done.23 = bf16[8,2,192,1024]{3,2,1,0:T(8,128)(2,1)} async-done(((bf16[8,2,192,1024]{3,2,1,0:T(8,128)(2,1)}), bf16[8,2,192,1024]{3,2,1,0:T(8,128)(2,1)}, u32[]{:S(2)}, u32[]{:S(2)}) %all-to-all-start.23) | async-done | bytes 6291488 | tf_op jit(solution)/shard_map/all_to_all | solution.py:36
  (545 shorter events, 1254.0 us)
Async XLA Ops:
  75.6 860.0 %collective-permute-start = (bf16[6,2,1024,1024]{3,2,1,0:T(8,128)(2,1)}, bf16[6,2,1024,1024]{3,2,1,0:T(8,128)(2,1)}, u32[]{:S(2)}, u32[]{:S(2)}) collective-permute-start(bf16[6,2,1024,1024]{3,2,1,0:T(8,128)(2,1)} %get-tuple-element.26), channel_id=1, source_target_pairs={{0,0},{1,2},{2,4},{3,6},{4,1},{5,3},{6,5},{7,7}} | collective-permute-start | bytes 75497480 | tf_op jit(solution)/shard_map/ppermute | solution.py:53
  264.7 707.7 %collective-permute-start.1 = (bf16[6,2,1024,1024]{3,2,1,0:T(8,128)(2,1)}, bf16[6,2,1024,1024]{3,2,1,0:T(8,128)(2,1)}, u32[]{:S(2)}, u32[]{:S(2)}) collective-permute-start(bf16[6,2,1024,1024]{3,2,1,0:T(8,128)(2,1)} %get-tuple-element.25), channel_id=1, source_target_pairs={{0,1},{1,3},{2,5},{3,7},{4,0},{5,2},{6,4},{7,6}} | collective-permute-start | bytes 75497480 | tf_op jit(solution)/shard_map/ppermute | solution.py:53
  282.2 150.6 %collective-permute-start.2 = (bf16[6,2,512,1024]{3,2,1,0:T(8,128)(2,1)}, bf16[6,2,512,1024]{3,2,1,0:T(8,128)(2,1)}, u32[]{:S(2)}, u32[]{:S(2)}) collective-permute-start(bf16[6,2,512,1024]{3,2,1,0:T(8,128)(2,1)} %get-tuple-element.28), channel_id=1, source_target_pairs={{0,0},{1,2},{2,4},{3,6},{4,1},{5,3},{6,5},{7,7}} | collective-permute-start | bytes 37748744 | tf_op jit(solution)/shard_map/ppermute | solution.py:54
  377.5 547.5 %collective-permute-start.3 = (bf16[6,2,512,1024]{3,2,1,0:T(8,128)(2,1)}, bf16[6,2,512,1024]{3,2,1,0:T(8,128)(2,1)}, u32[]{:S(2)}, u32[]{:S(2)}) collective-permute-start(bf16[6,2,512,1024]{3,2,1,0:T(8,128)(2,1)} %get-tuple-element.27), channel_id=1, source_target_pairs={{0,1},{1,3},{2,5},{3,7},{4,0},{5,2},{6,4},{7,6}} | collective-permute-start | bytes 37748744 | tf_op jit(solution)/shard_map/ppermute | solution.py:54
  428.5 564.6 %all-to-all-start = ((bf16[8,2,192,1024]{3,2,1,0:T(8,128)(2,1)}), bf16[8,2,192,1024]{3,2,1,0:T(8,128)(2,1)}, u32[]{:S(2)}, u32[]{:S(2)}) async-start(bf16[8,2,192,1024]{3,2,1,0:T(8,128)(2,1)} %bitcast.492), calls=%async_computation | async-start | bytes 12582912 | tf_op jit(solution)/shard_map/all_to_all | solution.py:32
  1018.0 82.6 %all-to-all-start.1 = ((bf16[8,2,192,1024]{3,2,1,0:T(8,128)(2,1)}), bf16[8,2,192,1024]{3,2,1,0:T(8,128)(2,1)}, u32[]{:S(2)}, u32[]{:S(2)}) async-start(bf16[8,2,192,1024]{3,2,1,0:T(8,128)(2,1)} %copy.98), calls=%async_computation.1 | async-start | bytes 12582912 | tf_op jit(solution)/shard_map/all_to_all | solution.py:36
  1120.4 209.8 %copy-start = (f32[256,1024]{1,0:T(8,128)}, f32[256,1024]{1,0:T(8,128)S(1)}, u32[]{:S(2)}) copy-start(f32[256,1024]{1,0:T(8,128)S(1)} %fusion.11) | copy-start | bytes 3145732
  1234.7 75.6 %all-to-all-start.3 = ((bf16[8,2,192,1024]{3,2,1,0:T(8,128)(2,1)}), bf16[8,2,192,1024]{3,2,1,0:T(8,128)(2,1)}, u32[]{:S(2)}, u32[]{:S(2)}) async-start(bf16[8,2,192,1024]{3,2,1,0:T(8,128)(2,1)} %copy.104), calls=%async_computation.3 | async-start | bytes 12582912 | tf_op jit(solution)/shard_map/all_to_all | solution.py:36
  1444.7 75.1 %all-to-all-start.5 = ((bf16[8,2,192,1024]{3,2,1,0:T(8,128)(2,1)}), bf16[8,2,192,1024]{3,2,1,0:T(8,128)(2,1)}, u32[]{:S(2)}, u32[]{:S(2)}) async-start(bf16[8,2,192,1024]{3,2,1,0:T(8,128)(2,1)} %copy.110), calls=%async_computation.5 | async-start | bytes 12582912 | tf_op jit(solution)/shard_map/all_to_all | solution.py:36
  1540.0 209.3 %copy-start.4 = (f32[256,1024]{1,0:T(8,128)}, f32[256,1024]{1,0:T(8,128)S(1)}, u32[]{:S(2)}) copy-start(f32[256,1024]{1,0:T(8,128)S(1)} %get-tuple-element.22) | copy-start | bytes 3145732
  1654.3 75.1 %all-to-all-start.7 = ((bf16[8,2,192,1024]{3,2,1,0:T(8,128)(2,1)}), bf16[8,2,192,1024]{3,2,1,0:T(8,128)(2,1)}, u32[]{:S(2)}, u32[]{:S(2)}) async-start(bf16[8,2,192,1024]{3,2,1,0:T(8,128)(2,1)} %copy.116), calls=%async_computation.7 | async-start | bytes 12582912 | tf_op jit(solution)/shard_map/all_to_all | solution.py:36
  1863.6 75.3 %all-to-all-start.9 = ((bf16[8,2,192,1024]{3,2,1,0:T(8,128)(2,1)}), bf16[8,2,192,1024]{3,2,1,0:T(8,128)(2,1)}, u32[]{:S(2)}, u32[]{:S(2)}) async-start(bf16[8,2,192,1024]{3,2,1,0:T(8,128)(2,1)} %copy.122), calls=%async_computation.9 | async-start | bytes 12582912 | tf_op jit(solution)/shard_map/all_to_all | solution.py:36
  1959.0 209.3 %copy-start.7 = (f32[256,1024]{1,0:T(8,128)}, f32[256,1024]{1,0:T(8,128)S(1)}, u32[]{:S(2)}) copy-start(f32[256,1024]{1,0:T(8,128)S(1)} %get-tuple-element.18) | copy-start | bytes 3145732
  2073.1 75.3 %all-to-all-start.11 = ((bf16[8,2,192,1024]{3,2,1,0:T(8,128)(2,1)}), bf16[8,2,192,1024]{3,2,1,0:T(8,128)(2,1)}, u32[]{:S(2)}, u32[]{:S(2)}) async-start(bf16[8,2,192,1024]{3,2,1,0:T(8,128)(2,1)} %copy.128), calls=%async_computation.11 | async-start | bytes 12582912 | tf_op jit(solution)/shard_map/all_to_all | solution.py:36
  2168.6 209.5 %copy-start.9 = (f32[256,1024]{1,0:T(8,128)}, f32[256,1024]{1,0:T(8,128)S(1)}, u32[]{:S(2)}) copy-start(f32[256,1024]{1,0:T(8,128)S(1)} %get-tuple-element.16) | copy-start | bytes 3145732
  2283.1 75.1 %all-to-all-start.13 = ((bf16[8,2,192,1024]{3,2,1,0:T(8,128)(2,1)}), bf16[8,2,192,1024]{3,2,1,0:T(8,128)(2,1)}, u32[]{:S(2)}, u32[]{:S(2)}) async-start(bf16[8,2,192,1024]{3,2,1,0:T(8,128)(2,1)} %copy.134), calls=%async_computation.13 | async-start | bytes 12582912 | tf_op jit(solution)/shard_map/all_to_all | solution.py:36
  2378.3 209.3 %copy-start.11 = (f32[256,1024]{1,0:T(8,128)}, f32[256,1024]{1,0:T(8,128)S(1)}, u32[]{:S(2)}) copy-start(f32[256,1024]{1,0:T(8,128)S(1)} %get-tuple-element.14) | copy-start | bytes 3145732
  2492.6 75.1 %all-to-all-start.15 = ((bf16[8,2,192,1024]{3,2,1,0:T(8,128)(2,1)}), bf16[8,2,192,1024]{3,2,1,0:T(8,128)(2,1)}, u32[]{:S(2)}, u32[]{:S(2)}) async-start(bf16[8,2,192,1024]{3,2,1,0:T(8,128)(2,1)} %copy.140), calls=%async_computation.15 | async-start | bytes 12582912 | tf_op jit(solution)/shard_map/all_to_all | solution.py:36
  2587.9 209.4 %copy-start.13 = (f32[256,1024]{1,0:T(8,128)}, f32[256,1024]{1,0:T(8,128)S(1)}, u32[]{:S(2)}) copy-start(f32[256,1024]{1,0:T(8,128)S(1)} %get-tuple-element.12) | copy-start | bytes 3145732
  2701.9 75.5 %all-to-all-start.17 = ((bf16[8,2,192,1024]{3,2,1,0:T(8,128)(2,1)}), bf16[8,2,192,1024]{3,2,1,0:T(8,128)(2,1)}, u32[]{:S(2)}, u32[]{:S(2)}) async-start(bf16[8,2,192,1024]{3,2,1,0:T(8,128)(2,1)} %copy.146), calls=%async_computation.17 | async-start | bytes 12582912 | tf_op jit(solution)/shard_map/all_to_all | solution.py:36
  2797.6 209.3 %copy-start.15 = (f32[256,1024]{1,0:T(8,128)}, f32[256,1024]{1,0:T(8,128)S(1)}, u32[]{:S(2)}) copy-start(f32[256,1024]{1,0:T(8,128)S(1)} %get-tuple-element.10) | copy-start | bytes 3145732
  2911.7 75.3 %all-to-all-start.19 = ((bf16[8,2,192,1024]{3,2,1,0:T(8,128)(2,1)}), bf16[8,2,192,1024]{3,2,1,0:T(8,128)(2,1)}, u32[]{:S(2)}, u32[]{:S(2)}) async-start(bf16[8,2,192,1024]{3,2,1,0:T(8,128)(2,1)} %copy.152), calls=%async_computation.19 | async-start | bytes 12582912 | tf_op jit(solution)/shard_map/all_to_all | solution.py:36
  3122.4 75.1 %all-to-all-start.21 = ((bf16[8,2,192,1024]{3,2,1,0:T(8,128)(2,1)}), bf16[8,2,192,1024]{3,2,1,0:T(8,128)(2,1)}, u32[]{:S(2)}, u32[]{:S(2)}) async-start(bf16[8,2,192,1024]{3,2,1,0:T(8,128)(2,1)} %copy.158), calls=%async_computation.21 | async-start | bytes 12582912 | tf_op jit(solution)/shard_map/all_to_all | solution.py:36
  3332.0 75.1 %all-to-all-start.23 = ((bf16[8,2,192,1024]{3,2,1,0:T(8,128)(2,1)}), bf16[8,2,192,1024]{3,2,1,0:T(8,128)(2,1)}, u32[]{:S(2)}, u32[]{:S(2)}) async-start(bf16[8,2,192,1024]{3,2,1,0:T(8,128)(2,1)} %copy.164), calls=%async_computation.23 | async-start | bytes 12582912 | tf_op jit(solution)/shard_map/all_to_all | solution.py:36
  (77 other events, 2496.9 us)
where the time goes:
time: 3460 us; the launch traced here: 3430 us
  waiting for transfers between devices  1170 us (34%)
  blocking collectives  803 us (23%)
  local copies, waits for them, and re-layouts  691 us (20%)
  starting transfers between devices  340 us (10%)
  matrix products  240 us (7%)
  other arithmetic  183 us (5%)
    all_to_all x11, blocking collectives, moe_layer(): inbound = lax.all_to_all(outbound, FLAT, 0, 0, tiled=True)  803 us
    all_to_all x12, waiting for transfers between devices, moe_layer(): returned = lax.all_to_all(expert_out, FLAT, 0, 0, tiled=True)  695 us
    ppermute x2, waiting for transfers between devices, hand_over(): lax.ppermute(lax.dynamic_slice_in_dim(down_loc, piece_idx * exp_dev, exp_...  473 us
    ppermute x2, starting transfers between devices, hand_over(): lax.ppermute(lax.dynamic_slice_in_dim(fused_loc, piece_idx * exp_dev, exp...  189 us
    gather x12, local copies, waits for them, and re-layouts, moe_layer(): jnp.take(returned.reshape(n_experts * capacity, model_width), slot_pos, a...  174 us
    gather x12, local copies, waits for them, and re-layouts, moe_layer(): jnp.take(normed, source_row, axis=0)  167 us
    dot_general x12, matrix products, moe_layer(): jnp.einsum('nxcd,xdg->nxcg', inbound, layer_w13, preferred_element_type=j...  136 us
    dot_general x12, matrix products, moe_layer(): jnp.einsum('nxcf,xfd->nxcd', activated, layer_down, preferred_element_typ...  104 us
  transfers between devices with their start and end apart: 17, of which 13 were waited for; matrix products, arithmetic and copies ran while one was open for 9% of the time, Pallas kernels for 0%

commit v1 on v0

v1 whole, which is shorter than its diff:
```python
import functools

import jax
import jax.numpy as jnp
from jax import lax
from jax.experimental import pallas as pl
from jax.experimental.pallas import tpu as pltpu
from jax.sharding import PartitionSpec as P

NORM_EPS = 1e-6
FLAT = ("stage", "expert")
MESH = pl.DeviceIdType.MESH
PART_A = 4


def moe_kernel(gate_hbm, up_hbm, down_hbm, x_vmem, mix_vmem, w13_hbm, wd_hbm, hid_hbm, w13_buf, wd_buf, u_buf, p_buf, r_buf, h_buf, g_buf, w_send, w_recv, load_sem, push_send, push_recv, u_send, u_recv, p_send, p_recv, g_send, g_recv, out_sem, credit):
    lay_stage, exp_grp = gate_hbm.shape[0], gate_hbm.shape[1]
    n_layers = hid_hbm.shape[0]
    ff = gate_hbm.shape[3]
    n_experts = exp_grp * 4
    sy = lax.axis_index("stage")
    sg = lax.axis_index("expert")
    sx, sc = sg // 2, sg % 2
    dst_y, dst_x = sx, sc
    partner = (sy, 2 * sx + 1 - sc)
    first_expert = 8 * sy + 4 * sx

    def peer(j):
        return ((sy + j // 2) % 2, 2 * ((sx + j % 2) % 2) + sc)

    def weight_parts(k, dst_core, j):
        layer = sy * lay_stage + k
        src_e = 2 * dst_core + j
        return (
            (gate_hbm.at[k, src_e], w13_hbm.at[layer, j, :, pl.ds(0, ff)]),
            (up_hbm.at[k, src_e], w13_hbm.at[layer, j, :, pl.ds(ff, ff)]),
            (down_hbm.at[k, src_e], wd_hbm.at[layer, j]),
        )

    def is_self(dst_core):
        return (dst_y == sy) & (2 * dst_x + dst_core == sg)

    def weight_remote(k, dst_core, j, i):
        src, dst = weight_parts(k, dst_core, j)[i]
        return pltpu.make_async_remote_copy(src, dst, w_send.at[k, dst_core, j, i], w_recv.at[sy * lay_stage + k, j, i], device_id=(dst_y, 2 * dst_x + dst_core), device_id_type=MESH)

    def weight_local(k, dst_core, j, i):
        src, dst = weight_parts(k, dst_core, j)[i]
        return pltpu.make_async_copy(src, dst, w_recv.at[sy * lay_stage + k, j, i])

    def send_weights(k, part_lo, part_hi):
        for idx in range(part_lo, part_hi):
            i, dst_core, j = idx % 3, (idx // 3) % 2, idx // 6

            @pl.when(is_self(dst_core))
            def _():
                weight_local(k, dst_core, j, i).start()

            @pl.when(jnp.logical_not(is_self(dst_core)))
            def _():
                weight_remote(k, dst_core, j, i).start()

    def landed(layer, j, i):
        dst = (w13_hbm.at[layer, j, :, pl.ds(0, ff)], w13_hbm.at[layer, j, :, pl.ds(ff, ff)], wd_hbm.at[layer, j])[i]
        src = (gate_hbm.at[0, 0], up_hbm.at[0, 0], down_hbm.at[0, 0])[i]
        return pltpu.make_async_copy(src, dst, w_recv.at[layer, j, i])

    def load_parts(layer, j):
        slot = layer % 2
        return (
            (w13_hbm.at[layer, j], w13_buf.at[slot, 2 * sc + j]),
            (wd_hbm.at[layer, j], wd_buf.at[slot, 2 * sc + j]),
        )

    def load_local(layer, j, i):
        src, dst = load_parts(layer, j)[i]
        return pltpu.make_async_copy(src, dst, load_sem.at[layer % 2, j, i])

    def load_push(layer, j, i):
        src, dst = load_parts(layer, j)[i]
        return pltpu.make_async_remote_copy(src, dst, push_send.at[layer % 2, j, i], push_recv.at[layer % 2, j, i], device_id=partner, device_id_type=MESH)

    def start_load(layer):
        @pl.when(layer >= 2)
        def _():
            pl.semaphore_wait(credit, 1)

        for j in range(2):
            for i in range(3):
                landed(layer, j, i).wait()
            for i in range(2):
                load_local(layer, j, i).start()
                load_push(layer, j, i).start()

    def finish_load(layer):
        for j in range(2):
            for i in range(2):
                load_local(layer, j, i).wait()
                load_push(layer, j, i).wait()

    def u_copy(j):
        return pltpu.make_async_remote_copy(u_buf.at[0], u_buf.at[j], u_send.at[j], u_recv.at[j], device_id=peer(j), device_id_type=MESH)

    def p_copy(j):
        return pltpu.make_async_remote_copy(p_buf.at[j], r_buf.at[j], p_send.at[j], p_recv.at[j], device_id=peer(j), device_id_type=MESH)

    def g_copy(j):
        return pltpu.make_async_remote_copy(mix_vmem, g_buf.at[j], g_send.at[j], g_recv.at[j], device_id=peer(j), device_id_type=MESH)

    def out_copy(layer):
        return pltpu.make_async_copy(h_buf.at[(layer + 1) % 2], hid_hbm.at[layer], out_sem.at[(layer + 1) % 2])

    for j in (1, 2, 3):
        g_copy(j).start()
    send_weights(0, 0, 12)
    h_buf[0] = x_vmem[...].astype(jnp.float32)
    g_buf[0] = mix_vmem[...]
    for j in (1, 2, 3):
        g_copy(j).wait()

    lane = lax.broadcasted_iota(jnp.int32, g_buf.shape[1:], 1)

    @pl.loop(0, n_layers)
    def _(layer):
        slot = layer % 2
        h = h_buf[slot]
        u_buf[0] = (h * lax.rsqrt(jnp.mean(h * h, axis=-1, keepdims=True) + NORM_EPS)).astype(jnp.bfloat16)
        for j in (1, 2, 3):
            u_copy(j).start()

        @pl.when(layer < lay_stage - 1)
        def _():
            send_weights(layer + 1, 0, PART_A)

        @pl.when(layer < lay_stage)
        def _():
            start_load(layer)

        finish_load(layer)

        @pl.loop(0, 4)
        def _(b):
            @pl.when(b > 0)
            def _():
                u_copy(b).wait()

            p_buf[b] = jnp.zeros(p_buf.shape[1:], jnp.float32)

            @pl.loop(0, exp_grp)
            def _(e):
                z = jnp.dot(u_buf[b], w13_buf[slot, e], preferred_element_type=jnp.float32)
                a = (jax.nn.silu(z[:, :ff]) * z[:, ff:]).astype(jnp.bfloat16)
                o = jnp.dot(a, wd_buf[slot, e], preferred_element_type=jnp.float32).astype(jnp.bfloat16).astype(jnp.float32)
                column = layer * n_experts + first_expert + e
                mix = jnp.sum(jnp.where(lane == column, g_buf[b], 0.0), axis=-1, keepdims=True)
                p_buf[b] = p_buf[b] + jnp.where(mix > 0.0, mix * o, 0.0)

            @pl.when(b > 0)
            def _():
                p_copy(b).start()

        @pl.when(layer < n_layers - 2)
        def _():
            pl.semaphore_signal(credit, 1, device_id=partner, device_id_type=MESH)

        @pl.when(layer < lay_stage - 1)
        def _():
            send_weights(layer + 1, PART_A, 12)

        @pl.when((layer >= lay_stage - 1) & (layer < n_layers - 1))
        def _():
            start_load(layer + 1)

        @pl.when(layer >= 2)
        def _():
            out_copy(layer - 2).wait()

        for j in (1, 2, 3):
            p_copy(j).wait()
        h_buf[1 - slot] = h_buf[slot] + (p_buf[0] + r_buf[1] + r_buf[2] + r_buf[3])
        out_copy(layer).start()

    out_copy(n_layers - 2).wait()
    out_copy(n_layers - 1).wait()

    @pl.loop(0, lay_stage)
    def _(k):
        for idx in range(12):
            i, dst_core, j = idx % 3, (idx // 3) % 2, idx // 6

            @pl.when(jnp.logical_not(is_self(dst_core)))
            def _():
                weight_remote(k, dst_core, j, i).wait_send()


def solution(mesh):
    n_stage = mesh.shape["stage"]
    n_group = mesh.shape["expert"]

    def per_device(gate_loc, up_loc, down_loc, x_loc, ids_loc, mix_loc):
        lay_stage, exp_grp, width, ff = gate_loc.shape
        n_layers, tok = ids_loc.shape[0], ids_loc.shape[1]
        n_experts = exp_grp * n_group
        exp_dev = exp_grp // n_stage
        onehot = ids_loc[..., None] == jnp.arange(n_experts, dtype=jnp.int32)
        dense = jnp.sum(jnp.where(onehot, mix_loc[..., None], 0.0), axis=2)
        dense = jnp.transpose(dense, (1, 0, 2)).reshape(tok, n_layers * n_experts)
        lanes = -(-dense.shape[1] // 128) * 128
        dense = jnp.pad(dense, ((0, 0), (0, lanes - dense.shape[1])))
        any_spec = pl.BlockSpec(memory_space=pl.ANY)
        vmem_spec = pl.BlockSpec(memory_space=pltpu.VMEM)
        dma = pltpu.SemaphoreType.DMA
        return pl.pallas_call(
            moe_kernel,
            out_shape=(
                jax.ShapeDtypeStruct((n_layers, exp_dev, width, 2 * ff), jnp.bfloat16),
                jax.ShapeDtypeStruct((n_layers, exp_dev, ff, width), jnp.bfloat16),
                jax.ShapeDtypeStruct((n_layers, tok, width), jnp.float32),
            ),
            in_specs=[any_spec, any_spec, any_spec, vmem_spec, vmem_spec],
            out_specs=(any_spec, any_spec, any_spec),
            scratch_shapes=[
                pltpu.VMEM((2, exp_grp, width, 2 * ff), jnp.bfloat16),
                pltpu.VMEM((2, exp_grp, ff, width), jnp.bfloat16),
                pltpu.VMEM((4, tok, width), jnp.bfloat16),
                pltpu.VMEM((4, tok, width), jnp.float32),
                pltpu.VMEM((4, tok, width), jnp.float32),
                pltpu.VMEM((2, tok, width), jnp.float32),
                pltpu.VMEM((4, tok, lanes), jnp.float32),
                dma((lay_stage, 2, 2, 3)),
                dma((n_layers, 2, 3)),
                dma((2, 2, 2)),
                dma((2, 2, 2)),
                dma((2, 2, 2)),
                dma((4,)),
                dma((4,)),
                dma((4,)),
                dma((4,)),
                dma((4,)),
                dma((4,)),
                dma((2,)),
                pltpu.SemaphoreType.REGULAR,
            ],
            compiler_params=pltpu.CompilerParams(has_side_effects=True, vmem_limit_bytes=60 * 1024 * 1024),
        )(gate_loc, up_loc, down_loc, x_loc, dense)

    weight_spec = P("stage", "expert")
    token_spec = P(None, FLAT)
    return jax.shard_map(per_device, mesh=mesh, in_specs=(weight_spec, weight_spec, weight_spec, P(FLAT), token_spec, token_spec), out_specs=(token_spec, token_spec, token_spec), check_vma=False)
```

time: 3460 us -> 1750 us (0.51)
  Pallas kernels: 0 us -> 1680 us
  waiting for transfers between devices: 1170 us -> 0 us
  blocking collectives: 803 us -> 0 us
  local copies, waits for them, and re-layouts: 691 us -> 67.4 us
  starting transfers between devices: 340 us -> 0 us
  matrix products: 240 us -> 0 us
  other arithmetic: 183 us -> 1.18 us
    pallas_call x0 -> x1, Pallas kernels: none -> 1680 us  [per_device(): pl.pallas_call(moe_kernel, out_shape=(jax.ShapeDtypeStruct((n_layers, exp...]
    all_to_all x11 -> x0, blocking collectives: 803 us -> none  [moe_layer(): inbound = lax.all_to_all(outbound, FLAT, 0, 0, tiled=True)]
    all_to_all x13 -> x0, waiting for transfers between devices: 695 us -> none  [the longest x12 695 us: moe_layer(): returned = lax.all_to_all(expert_out, FLAT, 0, 0, tiled=True)]
    ppermute x4 -> x0, waiting for transfers between devices: 473 us -> none  [the longest x2 473 us: hand_over(): lax.ppermute(lax.dynamic_slice_in_dim(down_loc, piece_idx * exp_dev, exp_...]
    gather x24 -> x0, local copies, waits for them, and re-layouts: 341 us -> none  [the longest x12 174 us: moe_layer(): jnp.take(returned.reshape(n_experts * capacity, model_width), slot_pos, a...]
    ppermute x4 -> x0, starting transfers between devices: 284 us -> none  [the longest x2 189 us: hand_over(): lax.ppermute(lax.dynamic_slice_in_dim(fused_loc, piece_idx * exp_dev, exp...]
    dot_general x24 -> x0, matrix products: 240 us -> none  [the longest x12 136 us: moe_layer(): jnp.einsum('nxcd,xdg->nxcg', inbound, layer_w13, preferred_element_type=j...]
    scatter x12 -> x0, local copies, waits for them, and re-layouts: 99 us -> none  [moe_layer(): jnp.zeros((n_experts * capacity,), jnp.int32).at[slot_pos].set(pair_tok)]
  transfers between devices with their start and end apart: 17 -> 0, of which waited for: 13 -> 0; matrix products, arithmetic and copies ran while one was open for 9% -> 0% of each run, Pallas kernels for 0% -> 0%
where the time goes in v1:
time: 1750 us
  Pallas kernels  1680 us (96%)
  local copies, waits for them, and re-layouts  67.4 us (4%)
    pallas_call x1, Pallas kernels, per_device(): pl.pallas_call(moe_kernel, out_shape=(jax.ShapeDtypeStruct((n_layers, exp...  1680 us
    unnamed x3, local copies, waits for them, and re-layouts  66.5 us

profile of v1, /device:TPU:0, one launch (start us, length us, event | category | flops | bytes accessed | tf_op | source)
XLA Modules:
  0.0 1746.4 jit_solution(16100518076172122795)
XLA Ops:
  0.6 1.2 select_reduce_fusion
  1.8 0.1 copy.14
  1.9 0.7 pad.4.mix_vmem
  2.7 1677.2 %shard_map.85 = (bf16[12,2,1024,1024]{3,2,1,0:T(8,128)(2,1)}, bf16[12,2,512,1024]{3,2,1,0:T(8,128)(2,1)}, f32[12,256,1024]{2,1,0:T(8,128)}) custom-call(bf16[6,4,1024,512]{3,2,1,0:T(8,128)(2,1)} %gate_hbm.1, bf16[6,4,1024,512]{3,2,1,0:T(8,128)(2,1)} %up_hbm.1, bf16[6,4,512,1024]{3,2,1,0:T(8,128)(2,1)} %down_hbm.1, bf16[256,1024]{1,0:T(8,128)(2,1)} %x_vmem.1, ...), custom_call_target="tpu_custom_call" | custom-call | tf_op jit(solution)/shard_map/pallas_call | solution.py:213
  1679.9 33.8 %copy.18 = bf16[12,2,1024,1024]{3,2,1,0:T(8,128)(2,1)} copy(bf16[12,2,1024,1024]{3,2,1,0:T(8,128)(2,1)} %get-tuple-element.6) | data formatting | bytes 100663296
  1713.7 20.6 %copy.19 = bf16[12,2,512,1024]{3,2,1,0:T(8,128)(2,1)} copy(bf16[12,2,512,1024]{3,2,1,0:T(8,128)(2,1)} %get-tuple-element.7) | data formatting | bytes 50331648
  1734.3 12.1 copy.20

commit v2 on v1

--- a/solution.py
+++ b/solution.py
@@ -10,10 +10,11 @@
 NORM_EPS = 1e-6
 FLAT = ("stage", "expert")
 MESH = pl.DeviceIdType.MESH
-PART_A = 4
-
-
-def moe_kernel(gate_hbm, up_hbm, down_hbm, x_vmem, mix_vmem, w13_hbm, wd_hbm, hid_hbm, w13_buf, wd_buf, u_buf, p_buf, r_buf, h_buf, g_buf, w_send, w_recv, load_sem, push_send, push_recv, u_send, u_recv, p_send, p_recv, g_send, g_recv, out_sem, credit):
+PART_A = 2
+QUARTERS = 2
+
+
+def moe_kernel(gate_hbm, up_hbm, down_hbm, x_vmem, mix_vmem, w13_hbm, wd_hbm, hid_hbm, w13_buf, wd_buf, u_buf, p_buf, r_buf, h_buf, g_buf, b13_buf, bd_buf, w_send, w_recv, load_sem, push_send, push_recv, u_send, u_recv, p_send, p_recv, g_send, g_recv, out_sem, credit):
     lay_stage, exp_grp = gate_hbm.shape[0], gate_hbm.shape[1]
     n_layers = hid_hbm.shape[0]
     ff = gate_hbm.shape[3]
@@ -25,8 +26,17 @@
     partner = (sy, 2 * sx + 1 - sc)
     first_expert = 8 * sy + 4 * sx
 
-    def peer(j):
-        return ((sy + j // 2) % 2, 2 * ((sx + j % 2) % 2) + sc)
+    half = u_buf.shape[1] // 2
+    quarter = half // QUARTERS
+
+    def neighbour(axis):
+        return ((sy, 2 * (1 - sx) + sc), (1 - sy, sg))[axis]
+
+    def rows(h):
+        return pl.ds(h * half, half)
+
+    def part(h, q):
+        return pl.ds(h * half + q * quarter, quarter)
 
     def weight_parts(k, dst_core, j):
         layer = sy * lay_stage + k
@@ -44,21 +54,44 @@
         src, dst = weight_parts(k, dst_core, j)[i]
         return pltpu.make_async_remote_copy(src, dst, w_send.at[k, dst_core, j, i], w_recv.at[sy * lay_stage + k, j, i], device_id=(dst_y, 2 * dst_x + dst_core), device_id_type=MESH)
 
-    def weight_local(k, dst_core, j, i):
-        src, dst = weight_parts(k, dst_core, j)[i]
-        return pltpu.make_async_copy(src, dst, w_recv.at[sy * lay_stage + k, j, i])
+    def bounce(j, i):
+        return (b13_buf.at[j, :, pl.ds(0, ff)], b13_buf.at[j, :, pl.ds(ff, ff)], bd_buf.at[j])[i]
+
+    def weight_read(k, dst_core, j, i):
+        return pltpu.make_async_copy(weight_parts(k, dst_core, j)[i][0], bounce(j, i), w_send.at[k, dst_core, j, i])
+
+    def weight_write(k, dst_core, j, i):
+        return pltpu.make_async_copy(bounce(j, i), weight_parts(k, dst_core, j)[i][1], w_recv.at[sy * lay_stage + k, j, i])
 
     def send_weights(k, part_lo, part_hi):
-        for idx in range(part_lo, part_hi):
-            i, dst_core, j = idx % 3, (idx // 3) % 2, idx // 6
+        parts = [(idx // 3 % 2, idx // 6, idx % 3) for idx in range(part_lo, part_hi)]
+        for dst_core, j, i in parts:
 
             @pl.when(is_self(dst_core))
             def _():
-                weight_local(k, dst_core, j, i).start()
+                weight_read(k, dst_core, j, i).start()
 
             @pl.when(jnp.logical_not(is_self(dst_core)))
             def _():
                 weight_remote(k, dst_core, j, i).start()
+
+        for core in (0, 1):
+
+            @pl.when(is_self(core))
+            def _():
+                for dst_core, j, i in parts:
+                    if dst_core == core:
+                        weight_read(k, dst_core, j, i).wait()
+                        weight_write(k, dst_core, j, i).start()
+
+    def finish_self(k):
+        for core in (0, 1):
+
+            @pl.when(is_self(core))
+            def _():
+                for j in range(2):
+                    for i in range(3):
+                        weight_write(k, core, j, i).wait()
 
     def landed(layer, j, i):
         dst = (w13_hbm.at[layer, j, :, pl.ds(0, ff)], w13_hbm.at[layer, j, :, pl.ds(ff, ff)], wd_hbm.at[layer, j])[i]
@@ -86,8 +119,11 @@
             pl.semaphore_wait(credit, 1)
 
         for j in range(2):
-            for i in range(3):
-                landed(layer, j, i).wait()
+            @pl.when(jnp.logical_not((layer // lay_stage == sy) & (2 * sy + sx == sg)))
+            def _():
+                for i in range(3):
+                    landed(layer, j, i).wait()
+
             for i in range(2):
                 load_local(layer, j, i).start()
                 load_push(layer, j, i).start()
@@ -98,25 +134,28 @@
                 load_local(layer, j, i).wait()
                 load_push(layer, j, i).wait()
 
-    def u_copy(j):
-        return pltpu.make_async_remote_copy(u_buf.at[0], u_buf.at[j], u_send.at[j], u_recv.at[j], device_id=peer(j), device_id_type=MESH)
-
-    def p_copy(j):
-        return pltpu.make_async_remote_copy(p_buf.at[j], r_buf.at[j], p_send.at[j], p_recv.at[j], device_id=peer(j), device_id_type=MESH)
-
-    def g_copy(j):
-        return pltpu.make_async_remote_copy(mix_vmem, g_buf.at[j], g_send.at[j], g_recv.at[j], device_id=peer(j), device_id_type=MESH)
+    def u_copy(t, h):
+        src = u_buf.at[1 if t == 3 else 0, rows(h)]
+        return pltpu.make_async_remote_copy(src, u_buf.at[t, rows(h)], u_send.at[t, h], u_recv.at[t, h], device_id=neighbour(h if t == 1 else 1 - h), device_id_type=MESH)
+
+    def p_copy(t, h, q):
+        return pltpu.make_async_remote_copy(p_buf.at[t, part(h, q)], r_buf.at[t, part(h, q)], p_send.at[t, h, q], p_recv.at[t, h, q], device_id=neighbour(1 - h if t == 2 else h), device_id_type=MESH)
+
+    def g_copy(t, h):
+        where = (1 - sy, 2 * (1 - sx) + sc) if t == 3 else neighbour(h if t == 1 else 1 - h)
+        return pltpu.make_async_remote_copy(mix_vmem.at[rows(h)], g_buf.at[t, rows(h)], g_send.at[t, h], g_recv.at[t, h], device_id=where, device_id_type=MESH)
 
     def out_copy(layer):
         return pltpu.make_async_copy(h_buf.at[(layer + 1) % 2], hid_hbm.at[layer], out_sem.at[(layer + 1) % 2])
 
-    for j in (1, 2, 3):
-        g_copy(j).start()
+    halves = [(t, h) for t in (1, 2, 3) for h in (0, 1)]
+    for t, h in halves:
+        g_copy(t, h).start()
     send_weights(0, 0, 12)
     h_buf[0] = x_vmem[...].astype(jnp.float32)
     g_buf[0] = mix_vmem[...]
-    for j in (1, 2, 3):
-        g_copy(j).wait()
+    for t, h in halves:
+        g_copy(t, h).wait()
 
     lane = lax.broadcasted_iota(jnp.int32, g_buf.shape[1:], 1)
 
@@ -125,24 +164,31 @@
         slot = layer % 2
         h = h_buf[slot]
         u_buf[0] = (h * lax.rsqrt(jnp.mean(h * h, axis=-1, keepdims=True) + NORM_EPS)).astype(jnp.bfloat16)
-        for j in (1, 2, 3):
-            u_copy(j).start()
-
-        @pl.when(layer < lay_stage - 1)
-        def _():
-            send_weights(layer + 1, 0, PART_A)
+        for t in (1, 2):
+            for h in (0, 1):
+                u_copy(t, h).start()
 
         @pl.when(layer < lay_stage)
         def _():
+            finish_self(layer)
             start_load(layer)
 
         finish_load(layer)
 
         @pl.loop(0, 4)
         def _(b):
-            @pl.when(b > 0)
-            def _():
-                u_copy(b).wait()
+            @pl.when(b == 1)
+            def _():
+                for h in (0, 1):
+                    u_copy(1, h).wait_recv()
+                    u_copy(3, h).start()
+
+            for t in (2, 3):
+
+                @pl.when(b == t)
+                def _():
+                    for h in (0, 1):
+                        u_copy(t, h).wait_recv()
 
             p_buf[b] = jnp.zeros(p_buf.shape[1:], jnp.float32)
 
@@ -155,9 +201,13 @@
                 mix = jnp.sum(jnp.where(lane == column, g_buf[b], 0.0), axis=-1, keepdims=True)
                 p_buf[b] = p_buf[b] + jnp.where(mix > 0.0, mix * o, 0.0)
 
-            @pl.when(b > 0)
-            def _():
-                p_copy(b).start()
+            for t in (1, 3):
+
+                @pl.when(b == t)
+                def _():
+                    for q in range(QUARTERS):
+                        for h in (0, 1):
+                            p_copy(t, h, q).start()
 
         @pl.when(layer < n_layers - 2)
         def _():
@@ -165,6 +215,18 @@
 
         @pl.when(layer < lay_stage - 1)
         def _():
+            send_weights(layer + 1, 0, PART_A)
+
+        for t, h in halves:
+            u_copy(t, h).wait_send()
+        for q in range(QUARTERS):
+            for h in (0, 1):
+                p_copy(3, h, q).wait_recv()
+                p_buf[2, part(h, q)] = p_buf[2, part(h, q)] + r_buf[3, part(h, q)]
+                p_copy(2, h, q).start()
+
+        @pl.when(layer < lay_stage - 1)
+        def _():
             send_weights(layer + 1, PART_A, 12)
 
         @pl.when((layer >= lay_stage - 1) & (layer < n_layers - 1))
@@ -175,9 +237,14 @@
         def _():
             out_copy(layer - 2).wait()
 
-        for j in (1, 2, 3):
-            p_copy(j).wait()
-        h_buf[1 - slot] = h_buf[slot] + (p_buf[0] + r_buf[1] + r_buf[2] + r_buf[3])
+        for q in range(QUARTERS):
+            for h in (0, 1):
+                p_copy(3, h, q).wait_send()
+                p_copy(1, h, q).wait()
+        for q in range(QUARTERS):
+            for h in (0, 1):
+                p_copy(2, h, q).wait()
+        h_buf[1 - slot] = h_buf[slot] + (p_buf[0] + r_buf[1] + r_buf[2])
         out_copy(layer).start()
 
     out_copy(n_layers - 2).wait()
@@ -191,6 +258,12 @@
             @pl.when(jnp.logical_not(is_self(dst_core)))
             def _():
                 weight_remote(k, dst_core, j, i).wait_send()
+
+
+def place_kernel(w13_in, wd_in, hid_in, w13_out, wd_out, hid_out):
+    w13_out[...] = w13_in[...]
+    wd_out[...] = wd_in[...]
+    hid_out[...] = hid_in[...]
 
 
 def solution(mesh):
@@ -210,7 +283,7 @@
         any_spec = pl.BlockSpec(memory_space=pl.ANY)
         vmem_spec = pl.BlockSpec(memory_space=pltpu.VMEM)
         dma = pltpu.SemaphoreType.DMA
-        return pl.pallas_call(
+        landed = pl.pallas_call(
             moe_kernel,
             out_shape=(
                 jax.ShapeDtypeStruct((n_layers, exp_dev, width, 2 * ff), jnp.bfloat16),
@@ -227,22 +300,35 @@
                 pltpu.VMEM((4, tok, width), jnp.float32),
                 pltpu.VMEM((2, tok, width), jnp.float32),
                 pltpu.VMEM((4, tok, lanes), jnp.float32),
+                pltpu.VMEM((exp_dev, width, 2 * ff), jnp.bfloat16),
+                pltpu.VMEM((exp_dev, ff, width), jnp.bfloat16),
                 dma((lay_stage, 2, 2, 3)),
                 dma((n_layers, 2, 3)),
                 dma((2, 2, 2)),
                 dma((2, 2, 2)),
                 dma((2, 2, 2)),
-                dma((4,)),
-                dma((4,)),
-                dma((4,)),
-                dma((4,)),
-                dma((4,)),
-                dma((4,)),
+                dma((4, 2)),
+                dma((4, 2)),
+                dma((4, 2, QUARTERS)),
+                dma((4, 2, QUARTERS)),
+                dma((4, 2)),
+                dma((4, 2)),
                 dma((2,)),
                 pltpu.SemaphoreType.REGULAR,
             ],
             compiler_params=pltpu.CompilerParams(has_side_effects=True, vmem_limit_bytes=60 * 1024 * 1024),
         )(gate_loc, up_loc, down_loc, x_loc, dense)
+        blocks = [(1, 1, width, 2 * ff), (1, 1, ff, width)]
+        specs = [pl.BlockSpec(block, lambda n: (n // exp_dev, n % exp_dev, 0, 0)) for block in blocks]
+        specs.append(pl.BlockSpec((1, tok // exp_dev, width), lambda n: (n // exp_dev, n % exp_dev, 0)))
+        return pl.pallas_call(
+            place_kernel,
+            out_shape=tuple(jax.ShapeDtypeStruct(one.shape, one.dtype) for one in landed),
+            grid=(n_layers * exp_dev,),
+            in_specs=specs,
+            out_specs=tuple(specs),
+            compiler_params=pltpu.CompilerParams(vmem_limit_bytes=60 * 1024 * 1024),
+        )(*landed)
 
     weight_spec = P("stage", "expert")
     token_spec = P(None, FLAT)

time: 1750 us -> 1540 us (0.88)
  Pallas kernels: 1680 us -> 1530 us
  local copies, waits for them, and re-layouts: 67.4 us -> 0.85 us
    pallas_call x1, Pallas kernels: 1680 us -> 1470 us  [per_device(): pl.pallas_call(moe_kernel, out_shape=(jax.ShapeDtypeStruct((n_layers, exp...]
    unnamed x3 -> x0, local copies, waits for them, and re-layouts: 66.5 us -> none
    pallas_call x0 -> x1, Pallas kernels: none -> 60.1 us  [per_device(): pl.pallas_call(place_kernel, out_shape=tuple((jax.ShapeDtypeStruct(one.sh...]
where the time goes in v2:
time: 1540 us; the launch traced here: 1530 us
  Pallas kernels  1530 us (99%)
    pallas_call x1, Pallas kernels, per_device(): pl.pallas_call(moe_kernel, out_shape=(jax.ShapeDtypeStruct((n_layers, exp...  1470 us
    pallas_call x1, Pallas kernels, per_device(): pl.pallas_call(place_kernel, out_shape=tuple((jax.ShapeDtypeStruct(one.sh...  60.1 us

profile of v2, /device:TPU:0, one launch (start us, length us, event | category | flops | bytes accessed | tf_op | source)
XLA Modules:
  0.0 1534.9 jit_solution(10178718215064951092)
XLA Ops:
  0.6 1.2 select_reduce_fusion
  1.8 0.1 copy.14
  1.9 0.7 pad.4.mix_vmem
  2.7 1472.2 %shard_map.85 = (bf16[12,2,1024,1024]{3,2,1,0:T(8,128)(2,1)}, bf16[12,2,512,1024]{3,2,1,0:T(8,128)(2,1)}, f32[12,256,1024]{2,1,0:T(8,128)}) custom-call(bf16[6,4,1024,512]{3,2,1,0:T(8,128)(2,1)} %gate_hbm.1, bf16[6,4,1024,512]{3,2,1,0:T(8,128)(2,1)} %up_hbm.1, bf16[6,4,512,1024]{3,2,1,0:T(8,128)(2,1)} %down_hbm.1, bf16[256,1024]{1,0:T(8,128)(2,1)} %x_vmem.1, ...), custom_call_target="tpu_custom_call" | custom-call | tf_op jit(solution)/shard_map/pallas_call | solution.py:286
  1474.8 60.1 %shard_map.86 = (bf16[12,2,1024,1024]{3,2,1,0:T(8,128)(2,1)}, bf16[12,2,512,1024]{3,2,1,0:T(8,128)(2,1)}, f32[12,256,1024]{2,1,0:T(8,128)}) custom-call(bf16[12,2,1024,1024]{3,2,1,0:T(8,128)(2,1)} %get-tuple-element.6.w13_in, bf16[12,2,512,1024]{3,2,1,0:T(8,128)(2,1)} %get-tuple-element.7.wd_in, f32[12,256,1024]{2,1,0:T(8,128)} %get-tuple-element.8.hid_in), custom_call_target="tpu_custom_call" | custom-call | tf_op jit(solution)/shard_map/pallas_call | solution.py:324
